TPU v7x, 32 devices: a whole 2x2x4 slice. The times are simulated.
32 devices in a mesh: groups: 2 (over y), batch: 4 (over z), blk: 4 (over x, core).
Axes of the slice: x: 2, y: 2, z: 4, core: 2. Of those that a mesh axis runs over, the one named last changes fastest.
Arguments:
- queries: bfloat16 [8, 592, 1024], P(('groups', 'batch'), 'blk'), parts along dimension 0, may hold values from -12 to 12
- key_states: bfloat16 [8, 592, 1024], P(('groups', 'batch'), 'blk'), parts along dimension 0, may hold values from -6 to 6
- value_states: bfloat16 [8, 592, 1024], P(('groups', 'batch'), 'blk'), parts along dimension 0, may hold values from -6 to 6
- residual: bfloat16 [8, 592, 768], P(('groups', 'batch'), 'blk'), parts along dimension 0, may hold values from -3 to 3
- proj_weight: bfloat16 [1024, 768], P(None, 'batch'), may hold values from -0.1875 to 0.1875
- conv_weight: bfloat16 [3, 3, 768, 384], P(None, None, 'batch'), may hold values from -0.078125 to 0.078125
Outputs:
- conv_out: bfloat16 [8, 592, 384], P(('groups', 'batch'), 'blk'), parts along dimension 0
There are 2 independent parts, one for each index of `groups`. A program takes and returns all parts, laid end to end along the dimension named above; an argument that names none is the same for every part. Nothing has to cross between parts.
All inputs are finite; a program needn't handle non-finite values.
Results may differ from a plain program's by a relative error of at most 0.0085.
Values may be sent and summed in bfloat16 or wider, within the bound.
A program may use at most 64 MiB of HBM per device.

v0:
```python
import jax
import jax.numpy as jnp
from jax import lax
from jax.sharding import PartitionSpec as P

HEADS = 16
HD = 64
COLS = 74
ROWS = 2


def extended(cells, sides, width):
    for axis, dim in sides:
        count = lax.axis_size(axis)
        ends = count - 1
        head = lax.slice_in_dim(cells, 0, width, axis=dim)
        tail = lax.slice_in_dim(cells, cells.shape[dim] - width, cells.shape[dim], axis=dim)
        cells = jnp.concatenate(
            [
                lax.ppermute(tail, axis, [(i, (i + 1) % count) for i in range(ends)]),
                cells,
                lax.ppermute(head, axis, [((i + 1) % count, i) for i in range(ends)]),
            ],
            axis=dim,
        )
    return cells


def empty_state(head_count, query_rows):
    return (
        jnp.full((head_count, query_rows), -1e30, jnp.float32),
        jnp.zeros((head_count, query_rows), jnp.float32),
        jnp.zeros((head_count, query_rows, HD), jnp.float32),
    )


def absorb(carry_state, query_block, key_block, value_block):
    row_max, weight_sum, running = carry_state
    scores = jnp.einsum(
        "qhd,khd->hqk", query_block, key_block, preferred_element_type=jnp.float32
    ) * HD ** (-0.5)
    new_max = jnp.maximum(row_max, jnp.max(scores, axis=2))
    factor = jnp.exp(row_max - new_max)
    weights = jnp.exp(scores - new_max[:, :, None])
    weight_sum = weight_sum * factor + jnp.sum(weights, axis=2)
    running = running * factor[:, :, None] + jnp.einsum(
        "hqk,khd->hqd",
        weights.astype(jnp.bfloat16),
        value_block,
        preferred_element_type=jnp.float32,
    )
    return (new_max, weight_sum, running)


def finish(carry_state):
    row_max, weight_sum, running = carry_state
    mixed = running / weight_sum[:, :, None]
    head_count, query_rows = weight_sum.shape
    return mixed.transpose(1, 0, 2).reshape(query_rows, head_count * HD).astype(jnp.bfloat16)


def body(queries, key_states, value_states, residual, proj_weight, conv_weight):
    query_rows = queries[0]
    key_rows = key_states[0]
    value_rows = value_states[0]
    tok_rows = query_rows.shape[0]
    cycle_count = lax.axis_size("blk")
    local_heads = HEADS // cycle_count
    query_all, key_all, value_all = (
        lax.all_to_all(query_rows, "blk", split_axis=1, concat_axis=0, tiled=True),
        lax.all_to_all(key_rows, "blk", split_axis=1, concat_axis=0, tiled=True),
        lax.all_to_all(value_rows, "blk", split_axis=1, concat_axis=0, tiled=True),
    )
    seq_rows = tok_rows * cycle_count
    group = 1
    while cycle_count % (group * 2) == 0 and tok_rows * group * 2 <= 1024:
        group = group * 2
    block_rows = tok_rows * group
    block_count = seq_rows // block_rows
    query_blocks = query_all.reshape(block_count, block_rows, local_heads, HD)
    key_blocks = key_all.reshape(block_count, block_rows, local_heads, HD)
    value_blocks = value_all.reshape(block_count, block_rows, local_heads, HD)

    def one_block(query_block):

        def absorb_one(index, inner_state):
            return absorb(inner_state, query_block, key_blocks[index], value_blocks[index])

        return finish(
            lax.fori_loop(0, block_count, absorb_one, empty_state(local_heads, block_rows))
        )

    mixed_rows = lax.map(one_block, query_blocks).reshape(seq_rows, local_heads * HD)
    attention = lax.all_to_all(mixed_rows, "blk", split_axis=0, concat_axis=1, tiled=True)
    projected = jnp.dot(
        attention,
        lax.all_gather(proj_weight, "batch", axis=1, tiled=True),
        preferred_element_type=jnp.float32,
    )
    hidden = (residual[0].astype(jnp.float32) + projected).astype(jnp.bfloat16)
    feature_grid = hidden.reshape(ROWS, COLS, hidden.shape[1])
    rimmed = extended(feature_grid, (("blk", 0),), 1)
    padded = jnp.pad(rimmed, ((0, 0), (1, 1), (0, 0)))
    shard_piece = lax.all_gather(conv_weight, "batch", axis=2, tiled=True)
    piece_rows = shard_piece.shape[2]
    windows = []
    for row_off in range(3):
        for col_off in range(3):
            windows.append(
                padded[row_off : row_off + ROWS, col_off : col_off + COLS].reshape(
                    tok_rows, piece_rows
                )
            )
    stacked = jnp.concatenate(windows, axis=1)
    flat_weight = shard_piece.reshape(9 * piece_rows, shard_piece.shape[3])
    conv_sum = jnp.dot(stacked, flat_weight, preferred_element_type=jnp.float32)
    return conv_sum.astype(jnp.bfloat16)[None]


def solution(mesh):
    return jax.shard_map(
        body,
        mesh=mesh,
        in_specs=(
            P(("groups", "batch"), "blk", None),
            P(("groups", "batch"), "blk", None),
            P(("groups", "batch"), "blk", None),
            P(("groups", "batch"), "blk", None),
            P(None, "batch"),
            P(None, None, "batch", None),
        ),
        out_specs=P(("groups", "batch"), "blk", None),
        check_vma=False,
    )
```

profile of v0, /device:TPU:0, one launch (start us, length us, event | category | flops | bytes accessed | tf_op | source)
XLA Modules:
  0.0 159.6 jit_solution(15283503268794246920)
XLA Ops:
  6.5 0.7 all-gather.3.cloned.1.call-update
  7.3 0.0 all-gather.5.cloned.1.call-start
  7.3 0.7 all-gather.5.cloned.1.call-update
  8.0 1.2 all_to_all.48
  9.2 0.7 copy.22
  9.9 4.2 %all-to-all-start = ((bf16[148,4,256]{2,0,1:T(8,128)(2,1)}), bf16[148,4,256]{2,0,1:T(8,128)(2,1)S(1)}, u32[]{:S(2)}, u32[]{:S(2)}) async-start(bf16[148,4,256]{2,0,1:T(8,128)(2,1)} %copy.22), calls=%async_computation | async-start | bytes 622592 | tf_op jit(solution)/shard_map/all_to_all | solution.py:70
  14.2 0.1 all_to_all.51
  14.3 0.8 copy.24
  15.1 5.6 %all-to-all-done = bf16[148,4,256]{2,0,1:T(8,128)(2,1)S(1)} async-done(((bf16[148,4,256]{2,0,1:T(8,128)(2,1)}), bf16[148,4,256]{2,0,1:T(8,128)(2,1)S(1)}, u32[]{:S(2)}, u32[]{:S(2)}) %all-to-all-start) | async-done | bytes 303136 | tf_op jit(solution)/shard_map/all_to_all | solution.py:70
  20.7 3.5 %all-to-all-start.1 = ((bf16[148,4,256]{2,0,1:T(8,128)(2,1)}), bf16[148,4,256]{2,0,1:T(8,128)(2,1)S(1)}, u32[]{:S(2)}, u32[]{:S(2)}) async-start(bf16[148,4,256]{2,0,1:T(8,128)(2,1)} %copy.24), calls=%async_computation.1 | async-start | bytes 622592 | tf_op jit(solution)/shard_map/all_to_all | solution.py:71
  24.2 0.1 all_to_all.54
  24.3 0.7 copy.26
  25.0 5.6 %all-to-all-done.1 = bf16[148,4,256]{2,0,1:T(8,128)(2,1)S(1)} async-done(((bf16[148,4,256]{2,0,1:T(8,128)(2,1)}), bf16[148,4,256]{2,0,1:T(8,128)(2,1)S(1)}, u32[]{:S(2)}, u32[]{:S(2)}) %all-to-all-start.1) | async-done | bytes 303136 | tf_op jit(solution)/shard_map/all_to_all | solution.py:71
  30.6 3.5 %all-to-all-start.2 = ((bf16[148,4,256]{2,0,1:T(8,128)(2,1)}), bf16[148,4,256]{2,0,1:T(8,128)(2,1)S(1)}, u32[]{:S(2)}, u32[]{:S(2)}) async-start(bf16[148,4,256]{2,0,1:T(8,128)(2,1)} %copy.26), calls=%async_computation.2 | async-start | bytes 622592 | tf_op jit(solution)/shard_map/all_to_all | solution.py:72
  34.1 0.3 reshape.91
  34.4 0.3 reshape.92
  34.7 5.9 %all-to-all-done.2 = bf16[148,4,256]{2,0,1:T(8,128)(2,1)S(1)} async-done(((bf16[148,4,256]{2,0,1:T(8,128)(2,1)}), bf16[148,4,256]{2,0,1:T(8,128)(2,1)S(1)}, u32[]{:S(2)}, u32[]{:S(2)}) %all-to-all-start.2) | async-done | bytes 303136 | tf_op jit(solution)/shard_map/all_to_all | solution.py:72
  40.6 0.3 reshape.93
  40.9 1.1 multiply_reduce_fusion
  42.0 1.0 fusion
  43.1 1.3 fusion.17
  44.4 0.4 convert_element_type.32
  44.8 0.3 copy.29
  45.1 8.9 %all_to_all.64 = bf16[4,148,256]{2,1,0:T(8,128)(2,1)S(1)} all-to-all(bf16[4,148,256]{2,1,0:T(8,128)(2,1)S(1)} %copy.29), channel_id=1, replica_groups=mesh['groups'=2,'batch'=4,'blk'=4] {'blk'}, dimensions={0} | all-to-all | bytes 606208 | tf_op jit(solution)/shard_map/all_to_all | solution.py:94
  54.0 0.1 copy.30
  54.1 0.1 pad.19
  54.3 0.0 all-gather.3.cloned.1.call-done
  54.3 2.2 %fusion.12 = bf16[148,768]{1,0:T(8,128)(2,1)S(1)} fusion(bf16[148,1024]{1,0:T(8,128)(2,1)S(1)} %bitcast.41, bf16[1024,768]{0,1:T(8,128)(2,1)} %all-gather.3.cloned.1.call-done, bf16[1,148,768]{2,1,0:T(8,128)(2,1)S(1)} %copy-done.2), kind=kOutput, calls=%fused_computation.12 | convolution fusion | flops 233124864 | bytes 2330624 | tf_op jit(solution)/shard_map/dot_general | solution.py:95
  56.5 1.7 %collective-permute-start = (bf16[1,74,768]{2,1,0:T(8,128)(2,1)S(1)}, bf16[1,74,768]{2,1,0:T(8,128)(2,1)S(1)}, u32[]{:S(2)}, u32[]{:S(2)}) collective-permute-start(bf16[1,74,768]{2,1,0:T(8,128)(2,1)S(1)} %get-tuple-element.60), channel_id=1, source_target_pairs={{0,1},{1,2},{2,3},{4,5},{5,6},{6,7},{8,9},{9,10},{10,11},{12,13},{... | collective-permute-start | bytes 341000 | tf_op jit(solution)/shard_map/ppermute | solution.py:20
  58.2 1.3 collective-permute-start.1
  59.5 0.1 reshape.80
  59.6 2.0 %collective-permute-done.1 = bf16[1,74,768]{2,1,0:T(8,128)(2,1)S(1)} collective-permute-done((bf16[1,74,768]{2,1,0:T(8,128)(2,1)S(1)}, bf16[1,74,768]{2,1,0:T(8,128)(2,1)S(1)}, u32[]{:S(2)}, u32[]{:S(2)}) %collective-permute-start.1) | collective-permute-done | bytes 113696 | tf_op jit(solution)/shard_map/ppermute | solution.py:22
  61.6 0.1 fusion.29
  61.7 0.1 fusion.31
  61.9 0.1 reshape.81
  61.9 0.1 pad_maximum_fusion
  62.0 0.8 reshape.82
  62.8 0.8 reshape.83
  63.5 0.8 reshape.84
  64.3 0.1 reshape.85
  64.3 0.1 reshape.86
  64.4 0.1 reshape.87
  64.4 0.1 reshape.88
  64.5 1.0 constant_dynamic-update-slice_fusion.7
  65.5 1.0 constant_dynamic-update-slice_fusion.6
  66.5 1.0 constant_dynamic-update-slice_fusion.5
  67.5 80.7 %all-gather.5.cloned.1.call-done = bf16[3,3,768,384]{3,2,1,0:T(8,128)(2,1)} async-done(((bf16[3,3,192,384]{3,2,1,0:T(8,128)(2,1)}), bf16[3,3,768,384]{3,2,1,0:T(8,128)(2,1)}) %all-gather.5.cloned.1.call-update) | async-done | bytes 5308432 | tf_op jit(solution)/shard_map/all_gather | solution.py:104
  148.3 4.5 %fusion.13 = bf16[1,148,384]{2,1,0:T(8,128)(2,1)} fusion(bf16[148,6912]{1,0:T(8,128)(2,1)S(1)} %constant_dynamic-update-slice_fusion, bf16[6912,384]{1,0:T(8,128)(2,1)} %bitcast.37), kind=kOutput, calls=%fused_computation.14 | convolution fusion | flops 785702400 | bytes 7468032 | tf_op jit(solution)/shard_map/dot_general | solution.py:116
  (18 shorter events, 0.2 us)
Async XLA Ops:
  6.5 7.6 %copy-start = (bf16[1,148,1024]{2,1,0:T(8,128)(2,1)S(1)}, bf16[1,148,1024]{2,1,0:T(8,128)(2,1)}, u32[]{:S(2)}) copy-start(bf16[1,148,1024]{2,1,0:T(8,128)(2,1)} %param.7) | copy-start | bytes 909316
  6.5 47.8 %all-gather.3.cloned.1.call-start = ((), (), s32[]{:S(2)}) async-start(), calls=%async_computation.4 | async-start | bytes 1966080 | tf_op jit(solution)/shard_map/all_gather | solution.py:97
  7.3 141.0 %all-gather.5.cloned.1.call-start = ((), (), s32[]{:S(2)}) async-start(), calls=%async_computation.5 | async-start | bytes 6635520 | tf_op jit(solution)/shard_map/all_gather | solution.py:104
  8.0 16.1 %copy-start.1 = (bf16[1,148,1024]{2,1,0:T(8,128)(2,1)S(1)}, bf16[1,148,1024]{2,1,0:T(8,128)(2,1)}, u32[]{:S(2)}) copy-start(bf16[1,148,1024]{2,1,0:T(8,128)(2,1)} %param.8) | copy-start | bytes 909316
  9.9 10.8 %all-to-all-start = ((bf16[148,4,256]{2,0,1:T(8,128)(2,1)}), bf16[148,4,256]{2,0,1:T(8,128)(2,1)S(1)}, u32[]{:S(2)}, u32[]{:S(2)}) async-start(bf16[148,4,256]{2,0,1:T(8,128)(2,1)} %copy.22), calls=%async_computation | async-start | bytes 622592 | tf_op jit(solution)/shard_map/all_to_all | solution.py:70
  20.7 10.0 %all-to-all-start.1 = ((bf16[148,4,256]{2,0,1:T(8,128)(2,1)}), bf16[148,4,256]{2,0,1:T(8,128)(2,1)S(1)}, u32[]{:S(2)}, u32[]{:S(2)}) async-start(bf16[148,4,256]{2,0,1:T(8,128)(2,1)} %copy.24), calls=%async_computation.1 | async-start | bytes 622592 | tf_op jit(solution)/shard_map/all_to_all | solution.py:71
  30.6 10.0 %all-to-all-start.2 = ((bf16[148,4,256]{2,0,1:T(8,128)(2,1)}), bf16[148,4,256]{2,0,1:T(8,128)(2,1)S(1)}, u32[]{:S(2)}, u32[]{:S(2)}) async-start(bf16[148,4,256]{2,0,1:T(8,128)(2,1)} %copy.26), calls=%async_computation.2 | async-start | bytes 622592 | tf_op jit(solution)/shard_map/all_to_all | solution.py:72
  44.4 9.9 %copy-start.2 = (bf16[1,148,768]{2,1,0:T(8,128)(2,1)S(1)}, bf16[1,148,768]{2,1,0:T(8,128)(2,1)}, u32[]{:S(2)}) copy-start(bf16[1,148,768]{2,1,0:T(8,128)(2,1)} %param.9) | copy-start | bytes 681988
  56.5 3.0 %collective-permute-start = (bf16[1,74,768]{2,1,0:T(8,128)(2,1)S(1)}, bf16[1,74,768]{2,1,0:T(8,128)(2,1)S(1)}, u32[]{:S(2)}, u32[]{:S(2)}) collective-permute-start(bf16[1,74,768]{2,1,0:T(8,128)(2,1)S(1)} %get-tuple-element.60), channel_id=1, source_target_pairs={{0,1},{1,2},{2,3},{4,5},{5,6},{6,7},{8,9},{9,10},{10,11},{12,13},{... | collective-permute-start | bytes 341000 | tf_op jit(solution)/shard_map/ppermute | solution.py:20
  58.2 3.4 %collective-permute-start.1 = (bf16[1,74,768]{2,1,0:T(8,128)(2,1)S(1)}, bf16[1,74,768]{2,1,0:T(8,128)(2,1)S(1)}, u32[]{:S(2)}, u32[]{:S(2)}) collective-permute-start(bf16[1,74,768]{2,1,0:T(8,128)(2,1)S(1)} %get-tuple-element.61), channel_id=1, source_target_pairs={{1,0},{2,1},{3,2},{5,4},{6,5},{7,6},{9,8},{10,9},{11,10},{13,12},{... | collective-permute-start | bytes 341000 | tf_op jit(solution)/shard_map/ppermute | solution.py:22
Sparse Core Ops, SparseCore 0:
  8.9 39.7 all-gather.2
  50.2 97.9 all-gather.4
where the time goes:
time: 160 us
  waiting for transfers between devices  101 us (63%)
  starting transfers between devices  14.1 us (9%)
  between operations  13.7 us (9%)
  local copies, waits for them, and re-layouts  11.2 us (7%)
  matrix products  9.04 us (6%)
  blocking collectives  8.9 us (6%)
    all_gather x1, waiting for transfers between devices, body(): shard_piece = lax.all_gather(conv_weight, 'batch', axis=2, tiled=True)  80.7 us
    all_to_all x1, blocking collectives, body(): lax.all_to_all(mixed_rows, 'blk', split_axis=0, concat_axis=1, tiled=True)  8.9 us
    all_to_all x1, waiting for transfers between devices, body(): lax.all_to_all(value_rows, 'blk', split_axis=1, concat_axis=0, tiled=True)  5.92 us
    all_to_all x1, waiting for transfers between devices, body(): lax.all_to_all(query_rows, 'blk', split_axis=1, concat_axis=0, tiled=True)  5.62 us
    all_to_all x1, waiting for transfers between devices, body(): lax.all_to_all(key_rows, 'blk', split_axis=1, concat_axis=0, tiled=True)  5.6 us
    dot_general x1, matrix products, body(): conv_sum = jnp.dot(stacked, flat_weight, preferred_element_type=jnp.float32)  4.48 us
    all_to_all x1, starting transfers between devices, body(): lax.all_to_all(query_rows, 'blk', split_axis=1, concat_axis=0, tiled=True)  4.24 us
    all_to_all x1, starting transfers between devices, body(): lax.all_to_all(value_rows, 'blk', split_axis=1, concat_axis=0, tiled=True)  3.45 us
  transfers between devices with their start and end apart: 7, of which 5 were waited for; matrix products, arithmetic and copies ran while one was open for 10% of the time, Pallas kernels for 0%

commit v1 on v0

--- a/solution.py
+++ b/solution.py
@@ -7,6 +7,17 @@
 HD = 64
 COLS = 74
 ROWS = 2
+
+
+def around_the_ring(x, axis, along):
+    size = lax.axis_size(axis)
+    right = [(i, (i + 1) % size) for i in range(size)]
+    terms = [x]
+    for far in range(1, size):
+        terms = [lax.ppermute(terms[0], axis, right), *terms]
+    whole = jnp.concatenate(terms, axis=along)
+    places = (lax.axis_index(axis) + 1) * terms[-1].shape[along]
+    return jnp.roll(whole, places, axis=along)
 
 
 def extended(cells, sides, width):
@@ -101,7 +112,7 @@
     feature_grid = hidden.reshape(ROWS, COLS, hidden.shape[1])
     rimmed = extended(feature_grid, (("blk", 0),), 1)
     padded = jnp.pad(rimmed, ((0, 0), (1, 1), (0, 0)))
-    shard_piece = lax.all_gather(conv_weight, "batch", axis=2, tiled=True)
+    shard_piece = around_the_ring(conv_weight, "batch", 2)
     piece_rows = shard_piece.shape[2]
     windows = []
     for row_off in range(3):

time: 160 us -> 177 us (1.11)
  local copies, waits for them, and re-layouts: 11.2 us -> 39.2 us
  waiting for transfers between devices: 101 us -> 85.3 us
  starting transfers between devices: 14.1 us -> 18.4 us
    all_gather x1 -> x0, waiting for transfers between devices: 80.7 us -> none  [body(): shard_piece = lax.all_gather(conv_weight, 'batch', axis=2, tiled=True)]
    ppermute x0 -> x3, waiting for transfers between devices: none -> 73.3 us  [around_the_ring(): terms = [lax.ppermute(terms[0], axis, right), *terms]]
    unnamed x16 -> x33, local copies, waits for them, and re-layouts: 3.14 us -> 12.8 us
    reshape x8, local copies, waits for them, and re-layouts: 2.53 us -> 11.8 us  [body(): padded[row_off:row_off + ROWS, col_off:col_off + COLS]]
    all_to_all x1, waiting for transfers between devices: 5.92 us -> 0.86 us  [body(): lax.all_to_all(value_rows, 'blk', split_axis=1, concat_axis=0, tiled=True)]
    dot_general x1, matrix products: 4.48 us -> 2.01 us  [body(): conv_sum = jnp.dot(stacked, flat_weight, preferred_element_type=jnp.float32)]
    ppermute x0 -> x3, starting transfers between devices: none -> 2.3 us  [around_the_ring(): terms = [lax.ppermute(terms[0], axis, right), *terms]]
    ppermute x1, waiting for transfers between devices: 2.01 us -> 0.01 us  [extended(): lax.ppermute(head, axis, [((i + 1) % count, i) for i in range(ends)])]
  transfers between devices with their start and end apart: 7 -> 9, of which waited for: 5 -> 7; matrix products, arithmetic and copies ran while one was open for 10% -> 20% of each run, Pallas kernels for 0% -> 0%
where the time goes in v1:
time: 177 us; the launch traced here: 176 us
  waiting for transfers between devices  85.3 us (48%)
  local copies, waits for them, and re-layouts  39.2 us (22%)
  starting transfers between devices  18.4 us (10%)
  between operations  13.7 us (8%)
  blocking collectives  9.11 us (5%)
  matrix products  7.56 us (4%)
  other arithmetic  2.97 us (2%)
    ppermute x3, waiting for transfers between devices, around_the_ring(): terms = [lax.ppermute(terms[0], axis, right), *terms]  73.3 us
    unnamed x33, local copies, waits for them, and re-layouts  12.8 us
    reshape x8, local copies, waits for them, and re-layouts, body(): padded[row_off:row_off + ROWS, col_off:col_off + COLS]  11.8 us
    all_to_all x1, blocking collectives, body(): lax.all_to_all(mixed_rows, 'blk', split_axis=0, concat_axis=1, tiled=True)  9.11 us
    all_to_all x1, waiting for transfers between devices, body(): lax.all_to_all(query_rows, 'blk', split_axis=1, concat_axis=0, tiled=True)  4.86 us
    all_to_all x1, waiting for transfers between devices, body(): lax.all_to_all(key_rows, 'blk', split_axis=1, concat_axis=0, tiled=True)  4.65 us
    all_to_all x1, starting transfers between devices, body(): lax.all_to_all(key_rows, 'blk', split_axis=1, concat_axis=0, tiled=True)  4.24 us
    all_to_all x1, starting transfers between devices, body(): lax.all_to_all(value_rows, 'blk', split_axis=1, concat_axis=0, tiled=True)  4.09 us
  transfers between devices with their start and end apart: 9, of which 7 were waited for; matrix products, arithmetic and copies ran while one was open for 20% of the time, Pallas kernels for 0%

profile of v1, /device:TPU:0, one launch (start us, length us, event | category | flops | bytes accessed | tf_op | source)
XLA Modules:
  0.0 176.3 jit_solution(636547361825307031)
XLA Ops:
  6.5 1.2 all_to_all.51
  7.8 0.8 copy.24
  8.5 4.2 %all-to-all-start.1 = ((bf16[148,4,256]{2,0,1:T(8,128)(2,1)}), bf16[148,4,256]{2,0,1:T(8,128)(2,1)S(1)}, u32[]{:S(2)}, u32[]{:S(2)}) async-start(bf16[148,4,256]{2,0,1:T(8,128)(2,1)} %copy.24), calls=%async_computation.1 | async-start | bytes 622592 | tf_op jit(solution)/shard_map/all_to_all | solution.py:82
  12.8 1.1 all_to_all.48
  13.9 0.8 copy.22
  14.7 4.6 %all-to-all-done.1 = bf16[148,4,256]{2,0,1:T(8,128)(2,1)S(1)} async-done(((bf16[148,4,256]{2,0,1:T(8,128)(2,1)}), bf16[148,4,256]{2,0,1:T(8,128)(2,1)S(1)}, u32[]{:S(2)}, u32[]{:S(2)}) %all-to-all-start.1) | async-done | bytes 303136 | tf_op jit(solution)/shard_map/all_to_all | solution.py:82
  19.3 3.5 %all-to-all-start = ((bf16[148,4,256]{2,0,1:T(8,128)(2,1)}), bf16[148,4,256]{2,0,1:T(8,128)(2,1)S(1)}, u32[]{:S(2)}, u32[]{:S(2)}) async-start(bf16[148,4,256]{2,0,1:T(8,128)(2,1)} %copy.22), calls=%async_computation | async-start | bytes 622592 | tf_op jit(solution)/shard_map/all_to_all | solution.py:81
  23.7 0.7 copy.26
  24.4 4.9 %all-to-all-done = bf16[148,4,256]{2,0,1:T(8,128)(2,1)S(1)} async-done(((bf16[148,4,256]{2,0,1:T(8,128)(2,1)}), bf16[148,4,256]{2,0,1:T(8,128)(2,1)S(1)}, u32[]{:S(2)}, u32[]{:S(2)}) %all-to-all-start) | async-done | bytes 303136 | tf_op jit(solution)/shard_map/all_to_all | solution.py:81
  29.3 0.7 copy-done.2
  30.0 4.1 %all-to-all-start.2 = ((bf16[148,4,256]{2,0,1:T(8,128)(2,1)}), bf16[148,4,256]{2,0,1:T(8,128)(2,1)}, u32[]{:S(2)}, u32[]{:S(2)}) async-start(bf16[148,4,256]{2,0,1:T(8,128)(2,1)} %copy.26), calls=%async_computation.2 | async-start | bytes 622592 | tf_op jit(solution)/shard_map/all_to_all | solution.py:83
  34.1 2.3 %collective-permute-start.2 = (bf16[3,3,192,384]{3,2,1,0:T(8,128)(2,1)S(1)}, bf16[3,3,192,384]{3,2,1,0:T(8,128)(2,1)S(1)}, u32[]{:S(2)}, u32[]{:S(2)}) collective-permute-start(bf16[3,3,192,384]{3,2,1,0:T(8,128)(2,1)S(1)} %copy-done), channel_id=1, source_target_pairs={{0,4},{4,8},{8,12},{12,0},{1,5},{5,9},{9,13},{13,1},{2,6},{6,10},{... | collective-permute-start | bytes 3981320 | tf_op jit(solution)/shard_map/ppermute | solution.py:17
  36.4 1.3 reshape.92
  37.7 2.1 %reshape.91 = bf16[592,4,64]{2,1,0:T(4,128)(2,1)} reshape(bf16[4,148,256]{2,1,0:T(8,128)(2,1)} %bitcast.39) | data formatting | bytes 606208 | tf_op jit(solution)/shard_map/while/body/jit(dynamic_index_in_dim)/squeeze | solution.py:104
  39.8 0.9 all-to-all-done.2
  40.7 2.1 %reshape.93 = bf16[592,4,64]{2,1,0:T(4,128)(2,1)} reshape(bf16[4,148,256]{2,1,0:T(8,128)(2,1)} %bitcast.4) | data formatting | bytes 606208 | tf_op jit(solution)/shard_map/while/body/eval_jaxpr/while/body/eval_jaxpr/squeeze | solution.py:98
  42.8 2.2 %multiply_reduce_fusion = (f32[4,592]{1,0:T(4,128)S(1)}, f32[4,592,592]{1,2,0:T(8,128)S(1)}) fusion(bf16[592,4,64]{2,1,0:T(4,128)(2,1)S(1)} %reshape.92, bf16[592,4,64]{2,1,0:T(4,128)(2,1)} %reshape.91), kind=kOutput, calls=%fused_computation.1 | convolution fusion | flops 182238912 | bytes 6223104 | tf_op jit(solution)/shard_map/while/body/eval_jaxpr/while/body/eval_jaxpr/qhd,khd->hqk/dot_general | solution.py:50
  45.0 1.0 fusion
  46.1 47.3 %collective-permute-done.2 = bf16[3,3,192,384]{3,2,1,0:T(8,128)(2,1)S(1)} collective-permute-done((bf16[3,3,192,384]{3,2,1,0:T(8,128)(2,1)S(1)}, bf16[3,3,192,384]{3,2,1,0:T(8,128)(2,1)S(1)}, u32[]{:S(2)}, u32[]{:S(2)}) %collective-permute-start.2) | collective-permute-done | bytes 1327136 | tf_op jit(solution)/shard_map/ppermute | solution.py:17
  93.4 1.3 fusion.17
  95.4 9.1 %all_to_all.64 = bf16[4,148,256]{2,1,0:T(8,128)(2,1)S(1)} all-to-all(bf16[4,148,256]{2,1,0:T(8,128)(2,1)S(1)} %copy.29), channel_id=1, replica_groups=mesh['groups'=2,'batch'=4,'blk'=4] {'blk'}, dimensions={0} | all-to-all | bytes 606208 | tf_op jit(solution)/shard_map/all_to_all | solution.py:105
  104.8 2.1 %fusion.12 = bf16[148,768]{1,0:T(8,128)(2,1)S(1)} fusion(bf16[148,1024]{1,0:T(8,128)(2,1)S(1)} %bitcast.40, bf16[1024,768]{0,1:T(8,128)(2,1)} %all-gather.2.cloned.1.call-done, bf16[1,148,768]{2,1,0:T(8,128)(2,1)} %param.9), kind=kOutput, calls=%fused_computation.12 | convolution fusion | flops 233124864 | bytes 2330624 | tf_op jit(solution)/shard_map/dot_general | solution.py:106
  107.6 1.3 collective-permute-start.1
  108.9 3.0 %collective-permute-start = (bf16[1,74,768]{2,1,0:T(8,128)(2,1)S(1)}, bf16[1,74,768]{2,1,0:T(8,128)(2,1)S(1)}, u32[]{:S(2)}, u32[]{:S(2)}) collective-permute-start(bf16[1,74,768]{2,1,0:T(8,128)(2,1)S(1)} %get-tuple-element.60), channel_id=1, source_target_pairs={{0,1},{1,2},{2,3},{4,5},{5,6},{6,7},{8,9},{9,10},{10,11},{12,13},{... | collective-permute-start | bytes 341000 | tf_op jit(solution)/shard_map/ppermute | solution.py:31
  112.0 0.9 collective-permute-done
  113.0 13.4 %collective-permute-done.3 = bf16[3,3,192,384]{3,2,1,0:T(8,128)(2,1)} collective-permute-done((bf16[3,3,192,384]{3,2,1,0:T(8,128)(2,1)S(1)}, bf16[3,3,192,384]{3,2,1,0:T(8,128)(2,1)}, u32[]{:S(2)}, u32[]{:S(2)}) %collective-permute-start.3) | collective-permute-done | bytes 1327136 | tf_op jit(solution)/shard_map/ppermute | solution.py:17
  126.4 1.1 fusion.31
  127.5 1.7 reshape.81
  129.2 1.8 pad_maximum_fusion
  131.0 1.7 reshape.82
  132.7 1.7 reshape.83
  134.3 1.7 reshape.84
  136.0 1.7 reshape.85
  137.7 1.0 reshape.86
  138.7 1.7 reshape.87
  140.4 0.7 reshape.88
  141.1 1.0 constant_dynamic-update-slice_fusion.8
  142.1 1.0 constant_dynamic-update-slice_fusion.7
  143.1 1.0 constant_dynamic-update-slice_fusion.6
  144.1 1.0 constant_dynamic-update-slice_fusion.5
  145.1 1.0 constant_dynamic-update-slice_fusion.3
  146.1 12.6 %collective-permute-done.4 = bf16[3,3,192,384]{3,2,1,0:T(8,128)(2,1)} collective-permute-done((bf16[3,3,192,384]{3,2,1,0:T(8,128)(2,1)}, bf16[3,3,192,384]{3,2,1,0:T(8,128)(2,1)}, u32[]{:S(2)}, u32[]{:S(2)}) %collective-permute-start.4) | collective-permute-done | bytes 1327136 | tf_op jit(solution)/shard_map/ppermute | solution.py:17
  158.8 1.5 constant_dynamic-update-slice_fusion.16
  160.2 1.6 constant_dynamic-update-slice_fusion.15
  162.4 1.6 constant_dynamic-update-slice_fusion.12
  164.0 1.6 constant_dynamic-update-slice_fusion.11
  166.1 1.3 constant_dynamic-slice_fusion
  167.4 2.0 %fusion.13 = bf16[1,148,384]{2,1,0:T(8,128)(2,1)} fusion(bf16[148,6912]{1,0:T(8,128)(2,1)S(1)} %constant_dynamic-update-slice_fusion, bf16[6912,384]{1,0:T(8,128)(2,1)S(1)} %bitcast.37), kind=kOutput, calls=%fused_computation.14 | convolution fusion | flops 785702400 | bytes 7468032 | tf_op jit(solution)/shard_map/dot_general | solution.py:127
  (40 shorter events, 3.9 us)
Async XLA Ops:
  6.5 17.0 %copy-start.7 = (bf16[1,148,1024]{2,1,0:T(8,128)(2,1)S(1)}, bf16[1,148,1024]{2,1,0:T(8,128)(2,1)}, u32[]{:S(2)}) copy-start(bf16[1,148,1024]{2,1,0:T(8,128)(2,1)} %param.8) | copy-start | bytes 909316
  6.5 27.5 %copy-start = (bf16[3,3,192,384]{3,2,1,0:T(8,128)(2,1)S(1)}, bf16[3,3,192,384]{3,2,1,0:T(8,128)(2,1)}, u32[]{:S(2)}) copy-start(bf16[3,3,192,384]{3,2,1,0:T(8,128)(2,1)} %param.11) | copy-start | bytes 3981316
  8.5 10.8 %all-to-all-start.1 = ((bf16[148,4,256]{2,0,1:T(8,128)(2,1)}), bf16[148,4,256]{2,0,1:T(8,128)(2,1)S(1)}, u32[]{:S(2)}, u32[]{:S(2)}) async-start(bf16[148,4,256]{2,0,1:T(8,128)(2,1)} %copy.24), calls=%async_computation.1 | async-start | bytes 622592 | tf_op jit(solution)/shard_map/all_to_all | solution.py:82
  19.3 17.1 %copy-start.1 = (bf16[148,4,256]{2,0,1:T(8,128)(2,1)}, bf16[148,4,256]{2,0,1:T(8,128)(2,1)S(1)}, u32[]{:S(2)}) copy-start(bf16[148,4,256]{2,0,1:T(8,128)(2,1)S(1)} %all-to-all-done.1) | copy-start | bytes 909316
  19.3 10.0 %all-to-all-start = ((bf16[148,4,256]{2,0,1:T(8,128)(2,1)}), bf16[148,4,256]{2,0,1:T(8,128)(2,1)S(1)}, u32[]{:S(2)}, u32[]{:S(2)}) async-start(bf16[148,4,256]{2,0,1:T(8,128)(2,1)} %copy.22), calls=%async_computation | async-start | bytes 622592 | tf_op jit(solution)/shard_map/all_to_all | solution.py:81
  22.8 82.1 %all-gather.2.cloned.1.call-start = ((), (), s32[]{:S(2)}) async-start(), calls=%async_computation.4 | async-start | bytes 1966080 | tf_op jit(solution)/shard_map/all_gather | solution.py:108
  29.3 0.7 copy-start.2
  30.0 10.7 %all-to-all-start.2 = ((bf16[148,4,256]{2,0,1:T(8,128)(2,1)}), bf16[148,4,256]{2,0,1:T(8,128)(2,1)}, u32[]{:S(2)}, u32[]{:S(2)}) async-start(bf16[148,4,256]{2,0,1:T(8,128)(2,1)} %copy.26), calls=%async_computation.2 | async-start | bytes 622592 | tf_op jit(solution)/shard_map/all_to_all | solution.py:83
  34.1 59.3 %collective-permute-start.2 = (bf16[3,3,192,384]{3,2,1,0:T(8,128)(2,1)S(1)}, bf16[3,3,192,384]{3,2,1,0:T(8,128)(2,1)S(1)}, u32[]{:S(2)}, u32[]{:S(2)}) collective-permute-start(bf16[3,3,192,384]{3,2,1,0:T(8,128)(2,1)S(1)} %copy-done), channel_id=1, source_target_pairs={{0,4},{4,8},{8,12},{12,0},{1,5},{5,9},{9,13},{13,1},{2,6},{6,10},{... | collective-permute-start | bytes 3981320 | tf_op jit(solution)/shard_map/ppermute | solution.py:17
  45.0 48.4 %copy-start.5 = (bf16[592,4,64]{2,1,0:T(4,128)(2,1)S(1)}, bf16[592,4,64]{2,1,0:T(4,128)(2,1)}, u32[]{:S(2)}) copy-start(bf16[592,4,64]{2,1,0:T(4,128)(2,1)} %reshape.93) | copy-start | bytes 909316
  93.4 33.0 %collective-permute-start.3 = (bf16[3,3,192,384]{3,2,1,0:T(8,128)(2,1)S(1)}, bf16[3,3,192,384]{3,2,1,0:T(8,128)(2,1)}, u32[]{:S(2)}, u32[]{:S(2)}) collective-permute-start(bf16[3,3,192,384]{3,2,1,0:T(8,128)(2,1)S(1)} %collective-permute-done.2), channel_id=1, source_target_pairs={{0,4},{4,8},{8,12},{12,0},{1,5},{5,9},{9,13},{13,1},{2,6},{6,10},{... | collective-permute-start | bytes 3981320 | tf_op jit(solution)/shard_map/ppermute | solution.py:17
  107.6 4.4 %collective-permute-start.1 = (bf16[1,74,768]{2,1,0:T(8,128)(2,1)}, bf16[1,74,768]{2,1,0:T(8,128)(2,1)S(1)}, u32[]{:S(2)}, u32[]{:S(2)}) collective-permute-start(bf16[1,74,768]{2,1,0:T(8,128)(2,1)} %get-tuple-element.61), channel_id=1, source_target_pairs={{1,0},{2,1},{3,2},{5,4},{6,5},{7,6},{9,8},{10,9},{11,10},{13,12},{... | collective-permute-start | bytes 341000 | tf_op jit(solution)/shard_map/ppermute | solution.py:33
  108.9 4.0 %collective-permute-start = (bf16[1,74,768]{2,1,0:T(8,128)(2,1)S(1)}, bf16[1,74,768]{2,1,0:T(8,128)(2,1)S(1)}, u32[]{:S(2)}, u32[]{:S(2)}) collective-permute-start(bf16[1,74,768]{2,1,0:T(8,128)(2,1)S(1)} %get-tuple-element.60), channel_id=1, source_target_pairs={{0,1},{1,2},{2,3},{4,5},{5,6},{6,7},{8,9},{9,10},{10,11},{12,13},{... | collective-permute-start | bytes 341000 | tf_op jit(solution)/shard_map/ppermute | solution.py:31
  112.9 13.5 %copy-start.6 = (bf16[1,74,768]{2,1,0:T(8,128)(2,1)}, bf16[1,74,768]{2,1,0:T(8,128)(2,1)S(1)}, u32[]{:S(2)}) copy-start(bf16[1,74,768]{2,1,0:T(8,128)(2,1)S(1)} %collective-permute-done) | copy-start | bytes 340996
  126.4 32.3 %collective-permute-start.4 = (bf16[3,3,192,384]{3,2,1,0:T(8,128)(2,1)}, bf16[3,3,192,384]{3,2,1,0:T(8,128)(2,1)}, u32[]{:S(2)}, u32[]{:S(2)}) collective-permute-start(bf16[3,3,192,384]{3,2,1,0:T(8,128)(2,1)} %collective-permute-done.3), channel_id=1, source_target_pairs={{0,4},{4,8},{8,12},{12,0},{1,5},{5,9},{9,13},{13,1},{2,6},{6,10},{... | collective-permute-start | bytes 3981320 | tf_op jit(solution)/shard_map/ppermute | solution.py:17
  141.1 4.9 %copy-start.3 = (bf16[148,768]{1,0:T(8,128)(2,1)S(1)}, bf16[148,768]{1,0:T(8,128)(2,1)}, u32[]{:S(2)}) copy-start(bf16[148,768]{1,0:T(8,128)(2,1)} %reshape.87) | copy-start | bytes 681988
  141.1 4.9 %copy-start.4 = (bf16[148,768]{1,0:T(8,128)(2,1)S(1)}, bf16[148,768]{1,0:T(8,128)(2,1)}, u32[]{:S(2)}) copy-start(bf16[148,768]{1,0:T(8,128)(2,1)} %reshape.88) | copy-start | bytes 681988
Sparse Core Ops, SparseCore 0:
  25.1 64.0 all-gather.1
